TPU v7x, 32 devices: a whole 2x2x4 slice. The times are simulated.
32 devices in a mesh: groups: 2 (over x), ctx: 16 (over z, y, core).
Axes of the slice: x: 2, y: 2, z: 4, core: 2. Of those that a mesh axis runs over, the one named last changes fastest.
Arguments:
- queries: bfloat16 [8192, 1024], P(('groups', 'ctx')), parts along dimension 0, may hold values from -7 to 7
- keys: bfloat16 [8192, 128], P(('groups', 'ctx')), parts along dimension 0, may hold values from -7 to 7
- values: bfloat16 [8192, 128], P(('groups', 'ctx')), parts along dimension 0, may hold values from -6 to 6
- span_order: int32 [64], P('groups'), parts along dimension 0, may hold values from 0 to 31, as said below
Outputs:
- attended: bfloat16 [8192, 1024], P(('groups', 'ctx')), parts along dimension 0
There are 2 independent parts, one for each index of `groups`. A program takes and returns all parts, laid end to end along the dimension named above; each array names one. Nothing has to cross between parts.
Inputs may be any that keep to these rules, and one draw needn't show every extreme that they name: A permutation: rows j * 128 to (j + 1) * 128 - 1 hold span span_order[j] of the sequence; for every j, span_order[2 j] + span_order[2 j + 1] = 31.
All inputs are finite; a program needn't handle non-finite values.
Results may differ from a plain program's by a relative error of at most 0.006.
Values may be sent and summed in bfloat16 or wider, within the bound.
No kernel may reach another device: no remote copies, remote signals or barrier semaphores. Data moves between devices by JAX's collectives and lax.ppermute only.
A program may use at most 64 MiB of HBM per device.

v0:
```python
import math
import jax
import jax.numpy as jnp
from jax import lax
from jax.sharding import PartitionSpec as P


def body(queries, keys, values, span_order):
    local_rows = queries.shape[0]
    head_size = keys.shape[1]
    heads = queries.shape[1] // head_size
    span = local_rows // 2
    device = lax.axis_index("ctx")
    key_positions = (
        span_order[:, None] * span + jnp.arange(span, dtype=jnp.int32)[None, :]
    ).reshape(-1)
    query_pos = lax.dynamic_slice_in_dim(key_positions, device * local_rows, local_rows, 0)
    query_heads = queries.reshape(local_rows, heads, head_size)
    scale = 1.0 / math.sqrt(head_size)

    def update(carry, key_blk, value_blk, key_pos):
        running, total, accum = carry
        score = (
            jnp.einsum("qhd,kd->hqk", query_heads, key_blk, preferred_element_type=jnp.float32)
            * scale
        )
        kept = key_pos[None, None, :] <= query_pos[None, :, None]
        score = jnp.where(kept, score, jnp.float32(-1e30))
        fresh = jnp.maximum(running, jnp.max(score, axis=-1))
        factor = jnp.exp(running - fresh)
        weight = jnp.where(kept, jnp.exp(score - fresh[:, :, None]), jnp.float32(0.0))
        total = total * factor + jnp.sum(weight, axis=-1)
        accum = accum * factor[:, :, None] + jnp.einsum(
            "hqk,kd->hqd",
            weight.astype(jnp.bfloat16),
            value_blk,
            preferred_element_type=jnp.float32,
        )
        return (fresh, total, accum)

    initial = (
        jnp.full((heads, local_rows), -1e30, jnp.float32),
        jnp.zeros((heads, local_rows), jnp.float32),
        jnp.zeros((heads, local_rows, head_size), jnp.float32),
    )
    key_piece = lax.all_gather(keys, "ctx", axis=0, tiled=True)
    value_piece = lax.all_gather(values, "ctx", axis=0, tiled=True)
    count = key_piece.shape[0]
    block = math.gcd(count, 512)

    def step(index, state):
        first = (index * block).astype(jnp.int32)
        key_blk = lax.dynamic_slice_in_dim(key_piece, first, block, 0)
        value_blk = lax.dynamic_slice_in_dim(value_piece, first, block, 0)
        key_pos = lax.dynamic_slice_in_dim(key_positions, first, block, 0)
        return update(state, key_blk, value_blk, key_pos)

    running, total, accum = lax.fori_loop(0, count // block, step, initial)
    mixed = accum / total[:, :, None]
    return (
        jnp.transpose(mixed, (1, 0, 2)).reshape(local_rows, heads * head_size).astype(jnp.bfloat16)
    )


def solution(mesh):
    in_specs = (
        P(("groups", "ctx"), None),
        P(("groups", "ctx"), None),
        P(("groups", "ctx"), None),
        P("groups"),
    )
    out_specs = P(("groups", "ctx"), None)
    return jax.shard_map(body, mesh=mesh, in_specs=in_specs, out_specs=out_specs, check_vma=False)
```

profile of v0, /device:TPU:0, one launch (start us, length us, event | category | flops | bytes accessed | tf_op | source)
XLA Modules:
  0.0 141.6 jit_solution(1959519106321978832)
XLA Ops:
  6.5 0.7 all-gather.3.cloned.1.call-update
  7.3 0.7 all-gather.5.cloned.1.call-update
  8.0 1.2 copy.8
  9.3 0.3 copy.9
  9.6 0.7 broadcast_multiply_fusion
  10.4 39.7 %all-gather.3.cloned.1.call-done = bf16[4096,128]{1,0:T(8,128)(2,1)} async-done(((bf16[256,128]{1,0:T(8,128)(2,1)}), bf16[4096,128]{1,0:T(8,128)(2,1)}) %all-gather.3.cloned.1.call-update) | async-done | bytes 1048592 | tf_op jit(solution)/shard_map/all_gather | solution.py:46
  50.1 39.0 %all-gather.5.cloned.1.call-done = bf16[4096,128]{1,0:T(8,128)(2,1)} async-done(((bf16[256,128]{1,0:T(8,128)(2,1)}), bf16[4096,128]{1,0:T(8,128)(2,1)}) %all-gather.5.cloned.1.call-update) | async-done | bytes 1048592 | tf_op jit(solution)/shard_map/all_gather | solution.py:47
  89.1 44.5 %while.18 = (s32[]{:T(128)}, f32[8,256]{1,0:T(8,128)S(1)}, f32[8,256]{1,0:T(8,128)S(1)}, f32[8,256,128]{2,1,0:T(8,128)S(1)}, s32[4096]{0:T(1024)S(1)}, /*index=5...) while((s32[]{:T(128)}, f32[8,256]{1,0:T(8,128)S(1)}, ...), condition=%wide.region_3.4_spmd.clone, body=%wide.region_0.3_spmd.clone.sunk | while | flops 551430144 | bytes 16129227 | solution.py:58
  89.2 0.1 broadcast_compare_fusion.2
  89.4 1.7 %fusion.33 = (f32[8,256]{1,0:T(8,128)S(1)}, f32[512,256,8]{1,0,2:T(8,128)S(1)}) fusion(pred[256,512]{0,1:T(8,128)(4,1)S(1)} %broadcast_compare_fusion.2, bf16[256,8,128]{2,0,1:T(8,128)(2,1)S(1)} %get-tuple-element.319, bf16[4096,128]{1,0:T(8,128)(2,1)} %get-tuple-element.318, s32[]{:T(128)S(6)} %select_n.62), kind=kOutput, calls=%fused_computation.2.clone.1 | convolution fusion | flops 271579136 | bytes 4988932 | tf_op jit(solution)/shard_map/while/body/eval_jaxpr/qhd,kd->hqk/dot_general | solution.py:24
  91.1 1.0 fusion.34
  92.1 2.6 %fusion.36 = f32[8,256,128]{2,1,0:T(8,128)S(1)} fusion(f32[512,256,8]{1,0,2:T(8,128)S(1)} %get-tuple-element.283, f32[8,256]{1,0:T(8,128)S(1)} %select_maximum_fusion.2, pred[256,512]{0,1:T(8,128)(4,1)S(1)} %broadcast_compare_fusion.2, f32[8,256,128]{2,1,0:T(8,128)S(1)} %get-tuple-element.302, f32[8,256]{1,0:T(8,128)S(1)} %get-tuple-element.285, ...), kind=kOutput, calls=%fused_computation.7.clone.1 | convolution fusion | flops 274464768 | bytes 6569989 | tf_op jit(solution)/shard_map/while/body/eval_jaxpr/hqk,kd->hqd/dot_general | solution.py:33
  94.7 0.1 dynamic_slice.43
  94.8 0.1 broadcast_compare_fusion.2
  94.9 1.7 %fusion.33 = (f32[8,256]{1,0:T(8,128)S(1)}, f32[512,256,8]{1,0,2:T(8,128)S(1)}) fusion(pred[256,512]{0,1:T(8,128)(4,1)S(1)} %broadcast_compare_fusion.2, bf16[256,8,128]{2,0,1:T(8,128)(2,1)S(1)} %get-tuple-element.319, bf16[4096,128]{1,0:T(8,128)(2,1)} %get-tuple-element.318, s32[]{:T(128)S(6)} %select_n.62), kind=kOutput, calls=%fused_computation.2.clone.1 | convolution fusion | flops 271579136 | bytes 4988932 | tf_op jit(solution)/shard_map/while/body/eval_jaxpr/qhd,kd->hqk/dot_general | solution.py:24
  96.6 1.0 fusion.34
  97.7 2.6 %fusion.36 = f32[8,256,128]{2,1,0:T(8,128)S(1)} fusion(f32[512,256,8]{1,0,2:T(8,128)S(1)} %get-tuple-element.283, f32[8,256]{1,0:T(8,128)S(1)} %select_maximum_fusion.2, pred[256,512]{0,1:T(8,128)(4,1)S(1)} %broadcast_compare_fusion.2, f32[8,256,128]{2,1,0:T(8,128)S(1)} %get-tuple-element.302, f32[8,256]{1,0:T(8,128)S(1)} %get-tuple-element.285, ...), kind=kOutput, calls=%fused_computation.7.clone.1 | convolution fusion | flops 274464768 | bytes 6569989 | tf_op jit(solution)/shard_map/while/body/eval_jaxpr/hqk,kd->hqd/dot_general | solution.py:33
  100.3 0.1 dynamic_slice.43
  100.3 0.1 broadcast_compare_fusion.2
  100.5 1.7 %fusion.33 = (f32[8,256]{1,0:T(8,128)S(1)}, f32[512,256,8]{1,0,2:T(8,128)S(1)}) fusion(pred[256,512]{0,1:T(8,128)(4,1)S(1)} %broadcast_compare_fusion.2, bf16[256,8,128]{2,0,1:T(8,128)(2,1)S(1)} %get-tuple-element.319, bf16[4096,128]{1,0:T(8,128)(2,1)} %get-tuple-element.318, s32[]{:T(128)S(6)} %select_n.62), kind=kOutput, calls=%fused_computation.2.clone.1 | convolution fusion | flops 271579136 | bytes 4988932 | tf_op jit(solution)/shard_map/while/body/eval_jaxpr/qhd,kd->hqk/dot_general | solution.py:24
  102.2 1.0 fusion.34
  103.2 2.6 %fusion.36 = f32[8,256,128]{2,1,0:T(8,128)S(1)} fusion(f32[512,256,8]{1,0,2:T(8,128)S(1)} %get-tuple-element.283, f32[8,256]{1,0:T(8,128)S(1)} %select_maximum_fusion.2, pred[256,512]{0,1:T(8,128)(4,1)S(1)} %broadcast_compare_fusion.2, f32[8,256,128]{2,1,0:T(8,128)S(1)} %get-tuple-element.302, f32[8,256]{1,0:T(8,128)S(1)} %get-tuple-element.285, ...), kind=kOutput, calls=%fused_computation.7.clone.1 | convolution fusion | flops 274464768 | bytes 6569989 | tf_op jit(solution)/shard_map/while/body/eval_jaxpr/hqk,kd->hqd/dot_general | solution.py:33
  105.8 0.1 dynamic_slice.43
  105.9 0.1 broadcast_compare_fusion.2
  106.1 1.7 %fusion.33 = (f32[8,256]{1,0:T(8,128)S(1)}, f32[512,256,8]{1,0,2:T(8,128)S(1)}) fusion(pred[256,512]{0,1:T(8,128)(4,1)S(1)} %broadcast_compare_fusion.2, bf16[256,8,128]{2,0,1:T(8,128)(2,1)S(1)} %get-tuple-element.319, bf16[4096,128]{1,0:T(8,128)(2,1)} %get-tuple-element.318, s32[]{:T(128)S(6)} %select_n.62), kind=kOutput, calls=%fused_computation.2.clone.1 | convolution fusion | flops 271579136 | bytes 4988932 | tf_op jit(solution)/shard_map/while/body/eval_jaxpr/qhd,kd->hqk/dot_general | solution.py:24
  107.8 1.0 fusion.34
  108.8 2.6 %fusion.36 = f32[8,256,128]{2,1,0:T(8,128)S(1)} fusion(f32[512,256,8]{1,0,2:T(8,128)S(1)} %get-tuple-element.283, f32[8,256]{1,0:T(8,128)S(1)} %select_maximum_fusion.2, pred[256,512]{0,1:T(8,128)(4,1)S(1)} %broadcast_compare_fusion.2, f32[8,256,128]{2,1,0:T(8,128)S(1)} %get-tuple-element.302, f32[8,256]{1,0:T(8,128)S(1)} %get-tuple-element.285, ...), kind=kOutput, calls=%fused_computation.7.clone.1 | convolution fusion | flops 274464768 | bytes 6569989 | tf_op jit(solution)/shard_map/while/body/eval_jaxpr/hqk,kd->hqd/dot_general | solution.py:33
  111.4 0.1 dynamic_slice.43
  111.5 0.1 broadcast_compare_fusion.2
  111.6 1.7 %fusion.33 = (f32[8,256]{1,0:T(8,128)S(1)}, f32[512,256,8]{1,0,2:T(8,128)S(1)}) fusion(pred[256,512]{0,1:T(8,128)(4,1)S(1)} %broadcast_compare_fusion.2, bf16[256,8,128]{2,0,1:T(8,128)(2,1)S(1)} %get-tuple-element.319, bf16[4096,128]{1,0:T(8,128)(2,1)} %get-tuple-element.318, s32[]{:T(128)S(6)} %select_n.62), kind=kOutput, calls=%fused_computation.2.clone.1 | convolution fusion | flops 271579136 | bytes 4988932 | tf_op jit(solution)/shard_map/while/body/eval_jaxpr/qhd,kd->hqk/dot_general | solution.py:24
  113.3 1.0 fusion.34
  114.4 2.6 %fusion.36 = f32[8,256,128]{2,1,0:T(8,128)S(1)} fusion(f32[512,256,8]{1,0,2:T(8,128)S(1)} %get-tuple-element.283, f32[8,256]{1,0:T(8,128)S(1)} %select_maximum_fusion.2, pred[256,512]{0,1:T(8,128)(4,1)S(1)} %broadcast_compare_fusion.2, f32[8,256,128]{2,1,0:T(8,128)S(1)} %get-tuple-element.302, f32[8,256]{1,0:T(8,128)S(1)} %get-tuple-element.285, ...), kind=kOutput, calls=%fused_computation.7.clone.1 | convolution fusion | flops 274464768 | bytes 6569989 | tf_op jit(solution)/shard_map/while/body/eval_jaxpr/hqk,kd->hqd/dot_general | solution.py:33
  117.0 0.1 dynamic_slice.43
  117.0 0.1 broadcast_compare_fusion.2
  117.2 1.7 %fusion.33 = (f32[8,256]{1,0:T(8,128)S(1)}, f32[512,256,8]{1,0,2:T(8,128)S(1)}) fusion(pred[256,512]{0,1:T(8,128)(4,1)S(1)} %broadcast_compare_fusion.2, bf16[256,8,128]{2,0,1:T(8,128)(2,1)S(1)} %get-tuple-element.319, bf16[4096,128]{1,0:T(8,128)(2,1)} %get-tuple-element.318, s32[]{:T(128)S(6)} %select_n.62), kind=kOutput, calls=%fused_computation.2.clone.1 | convolution fusion | flops 271579136 | bytes 4988932 | tf_op jit(solution)/shard_map/while/body/eval_jaxpr/qhd,kd->hqk/dot_general | solution.py:24
  118.9 1.0 fusion.34
  119.9 2.6 %fusion.36 = f32[8,256,128]{2,1,0:T(8,128)S(1)} fusion(f32[512,256,8]{1,0,2:T(8,128)S(1)} %get-tuple-element.283, f32[8,256]{1,0:T(8,128)S(1)} %select_maximum_fusion.2, pred[256,512]{0,1:T(8,128)(4,1)S(1)} %broadcast_compare_fusion.2, f32[8,256,128]{2,1,0:T(8,128)S(1)} %get-tuple-element.302, f32[8,256]{1,0:T(8,128)S(1)} %get-tuple-element.285, ...), kind=kOutput, calls=%fused_computation.7.clone.1 | convolution fusion | flops 274464768 | bytes 6569989 | tf_op jit(solution)/shard_map/while/body/eval_jaxpr/hqk,kd->hqd/dot_general | solution.py:33
  122.5 0.1 dynamic_slice.43
  122.6 0.1 broadcast_compare_fusion.2
  122.8 1.7 %fusion.33 = (f32[8,256]{1,0:T(8,128)S(1)}, f32[512,256,8]{1,0,2:T(8,128)S(1)}) fusion(pred[256,512]{0,1:T(8,128)(4,1)S(1)} %broadcast_compare_fusion.2, bf16[256,8,128]{2,0,1:T(8,128)(2,1)S(1)} %get-tuple-element.319, bf16[4096,128]{1,0:T(8,128)(2,1)} %get-tuple-element.318, s32[]{:T(128)S(6)} %select_n.62), kind=kOutput, calls=%fused_computation.2.clone.1 | convolution fusion | flops 271579136 | bytes 4988932 | tf_op jit(solution)/shard_map/while/body/eval_jaxpr/qhd,kd->hqk/dot_general | solution.py:24
  124.5 1.0 fusion.34
  125.5 2.6 %fusion.36 = f32[8,256,128]{2,1,0:T(8,128)S(1)} fusion(f32[512,256,8]{1,0,2:T(8,128)S(1)} %get-tuple-element.283, f32[8,256]{1,0:T(8,128)S(1)} %select_maximum_fusion.2, pred[256,512]{0,1:T(8,128)(4,1)S(1)} %broadcast_compare_fusion.2, f32[8,256,128]{2,1,0:T(8,128)S(1)} %get-tuple-element.302, f32[8,256]{1,0:T(8,128)S(1)} %get-tuple-element.285, ...), kind=kOutput, calls=%fused_computation.7.clone.1 | convolution fusion | flops 274464768 | bytes 6569989 | tf_op jit(solution)/shard_map/while/body/eval_jaxpr/hqk,kd->hqd/dot_general | solution.py:33
  128.1 0.1 dynamic_slice.43
  128.2 0.1 broadcast_compare_fusion.2
  128.3 1.7 %fusion.33 = (f32[8,256]{1,0:T(8,128)S(1)}, f32[512,256,8]{1,0,2:T(8,128)S(1)}) fusion(pred[256,512]{0,1:T(8,128)(4,1)S(1)} %broadcast_compare_fusion.2, bf16[256,8,128]{2,0,1:T(8,128)(2,1)S(1)} %get-tuple-element.319, bf16[4096,128]{1,0:T(8,128)(2,1)} %get-tuple-element.318, s32[]{:T(128)S(6)} %select_n.62), kind=kOutput, calls=%fused_computation.2.clone.1 | convolution fusion | flops 271579136 | bytes 4988932 | tf_op jit(solution)/shard_map/while/body/eval_jaxpr/qhd,kd->hqk/dot_general | solution.py:24
  130.0 1.0 fusion.34
  131.1 2.6 %fusion.36 = f32[8,256,128]{2,1,0:T(8,128)S(1)} fusion(f32[512,256,8]{1,0,2:T(8,128)S(1)} %get-tuple-element.283, f32[8,256]{1,0:T(8,128)S(1)} %select_maximum_fusion.2, pred[256,512]{0,1:T(8,128)(4,1)S(1)} %broadcast_compare_fusion.2, f32[8,256,128]{2,1,0:T(8,128)S(1)} %get-tuple-element.302, f32[8,256]{1,0:T(8,128)S(1)} %get-tuple-element.285, ...), kind=kOutput, calls=%fused_computation.7.clone.1 | convolution fusion | flops 274464768 | bytes 6569989 | tf_op jit(solution)/shard_map/while/body/eval_jaxpr/hqk,kd->hqd/dot_general | solution.py:33
  133.7 1.1 copy_bitcast_fusion
  (32 shorter events, 0.4 us)
Async XLA Ops:
  6.5 43.6 %all-gather.3.cloned.1.call-start = ((), (), s32[]{:S(2)}) async-start(), calls=%async_computation | async-start | bytes 1114112 | tf_op jit(solution)/shard_map/all_gather | solution.py:46
  7.3 81.9 %all-gather.5.cloned.1.call-start = ((), (), s32[]{:S(2)}) async-start(), calls=%async_computation.1 | async-start | bytes 1114112 | tf_op jit(solution)/shard_map/all_gather | solution.py:47
Sparse Core Ops, SparseCore 0:
  9.5 40.5 all-gather.2
  52.3 36.8 all-gather.4
where the time goes:
time: 142 us
  waiting for transfers between devices  80.2 us (56%)
  matrix products  33.9 us (24%)
  between operations  13.5 us (10%)
  other arithmetic  11.2 us (8%)
  local copies, waits for them, and re-layouts  2.23 us (2%)
    all_gather x1, waiting for transfers between devices, body(): key_piece = lax.all_gather(keys, 'ctx', axis=0, tiled=True)  39.7 us
    all_gather x1, waiting for transfers between devices, body(): value_piece = lax.all_gather(values, 'ctx', axis=0, tiled=True)  39 us
    dot_general x8, matrix products, update(): jnp.einsum('hqk,kd->hqd', weight.astype(jnp.bfloat16), value_blk, preferr...  20.4 us
    dot_general x8, matrix products, update(): jnp.einsum('qhd,kd->hqk', query_heads, key_blk, preferred_element_type=jn...  13.5 us
    reduce_sum x8, other arithmetic, update(): total = total * factor + jnp.sum(weight, axis=-1)  8.06 us
  transfers between devices with their start and end apart: 2, of which 2 were waited for; matrix products, arithmetic and copies ran while one was open for 2% of the time, Pallas kernels for 0%

commit v1 on v0

--- a/solution.py
+++ b/solution.py
@@ -43,8 +43,13 @@
         jnp.zeros((heads, local_rows), jnp.float32),
         jnp.zeros((heads, local_rows, head_size), jnp.float32),
     )
-    key_piece = lax.all_gather(keys, "ctx", axis=0, tiled=True)
-    value_piece = lax.all_gather(values, "ctx", axis=0, tiled=True)
+
+    def follow_the_slot(vec, mine_x, along_axis):
+        far_arr = jnp.concatenate([vec, mine_x], 1)
+        last = lax.all_gather(far_arr, along_axis, axis=0, tiled=True)
+        return jnp.split(last, [vec.shape[1]], 1)
+
+    key_piece, value_piece = follow_the_slot(keys, values, "ctx")
     count = key_piece.shape[0]
     block = math.gcd(count, 512)
 

time: 142 us -> 102 us (0.72)
  waiting for transfers between devices: 80.2 us -> 43.2 us
  matrix products: 33.9 us -> 26.7 us
  local copies, waits for them, and re-layouts: 2.23 us -> 4.9 us
  other arithmetic: 11.2 us -> 12.8 us
    all_gather x2 -> x1, waiting for transfers between devices: 78.8 us -> 43.2 us  [follow_the_slot(): last = lax.all_gather(far_arr, along_axis, axis=0, tiled=True)]
    dot_general x8, matrix products: 13.5 us -> 6.24 us  [update(): jnp.einsum('qhd,kd->hqk', query_heads, key_blk, preferred_element_type=jn...]
    split x0 -> x1, local copies, waits for them, and re-layouts: none -> 2.66 us  [follow_the_slot(): return jnp.split(last, [vec.shape[1]], 1)]
    concatenate x0 -> x1, other arithmetic: none -> 1.54 us  [follow_the_slot(): far_arr = jnp.concatenate([vec, mine_x], 1)]
  transfers between devices with their start and end apart: 2 -> 1, of which waited for: 2 -> 1; matrix products, arithmetic and copies ran while one was open for 2% -> 2% of each run, Pallas kernels for 0% -> 0%
where the time goes in v1:
time: 102 us
  waiting for transfers between devices  43.2 us (42%)
  matrix products  26.7 us (26%)
  between operations  13.4 us (13%)
  other arithmetic  12.8 us (13%)
  local copies, waits for them, and re-layouts  4.9 us (5%)
    all_gather x1, waiting for transfers between devices, follow_the_slot(): last = lax.all_gather(far_arr, along_axis, axis=0, tiled=True)  43.2 us
    dot_general x8, matrix products, update(): jnp.einsum('hqk,kd->hqd', weight.astype(jnp.bfloat16), value_blk, preferr...  20.4 us
    reduce_sum x8, other arithmetic, update(): total = total * factor + jnp.sum(weight, axis=-1)  8.06 us
    dot_general x8, matrix products, update(): jnp.einsum('qhd,kd->hqk', query_heads, key_blk, preferred_element_type=jn...  6.24 us
    split x1, local copies, waits for them, and re-layouts, follow_the_slot(): return jnp.split(last, [vec.shape[1]], 1)  2.66 us
  transfers between devices with their start and end apart: 1, of which 1 were waited for; matrix products, arithmetic and copies ran while one was open for 2% of the time, Pallas kernels for 0%

profile of v1, /device:TPU:0, one launch (start us, length us, event | category | flops | bytes accessed | tf_op | source)
XLA Modules:
  0.0 101.6 jit_solution(2815374030676099759)
XLA Ops:
  6.5 1.5 %pad_maximum_fusion = bf16[256,256]{1,0:T(8,128)(2,1)} fusion(bf16[256,128]{1,0:T(8,128)(2,1)} %param.8, bf16[256,128]{1,0:T(8,128)(2,1)} %param.7), kind=kLoop, calls=%fused_computation.27 | loop fusion | flops 262144 | bytes 262144 | tf_op jit(solution)/shard_map/concatenate | solution.py:48
  8.1 1.2 %copy.8 = bf16[256,1024]{0,1:T(8,128)(2,1)S(1)} copy(bf16[256,1024]{1,0:T(8,128)(2,1)} %param.6) | data formatting | bytes 1048576 | tf_op args[0]
  9.4 0.3 copy.9
  9.7 0.7 broadcast_multiply_fusion
  10.5 43.2 %all-gather.2.cloned.1.call-done = bf16[4096,256]{1,0:T(8,128)(2,1)} async-done(((bf16[256,256]{1,0:T(8,128)(2,1)}), bf16[4096,256]{1,0:T(8,128)(2,1)}) %all-gather.2.cloned.1.call-update) | async-done | bytes 2097168 | tf_op jit(solution)/shard_map/all_gather | solution.py:49
  53.7 2.7 %fusion.21 = (bf16[4096,128]{1,0:T(8,128)(2,1)}, bf16[4096,128]{1,0:T(8,128)(2,1)S(1)}) fusion(bf16[4096,256]{1,0:T(8,128)(2,1)} %all-gather.2.cloned.1.call-done), kind=kLoop, calls=%fused_computation.30 | loop fusion | bytes 4194304 | tf_op jit(solution)/shard_map/split | solution.py:50
  56.4 37.2 %while.18 = (s32[]{:T(128)}, f32[8,256]{1,0:T(8,128)S(1)}, f32[8,256]{1,0:T(8,128)S(1)}, f32[8,256,128]{2,1,0:T(8,128)S(1)}, s32[4096]{0:T(1024)S(1)}, /*index=5...) while((s32[]{:T(128)}, f32[8,256]{1,0:T(8,128)S(1)}, ...), condition=%wide.region_3.4_spmd.clone, body=%wide.region_0.3_spmd.clone.sunk | while | flops 551430144 | bytes 16129227 | solution.py:63
  56.4 0.1 dynamic_slice.43
  56.4 0.1 broadcast_compare_fusion.2
  56.6 0.8 fusion.34
  57.4 1.0 fusion.35
  58.4 2.6 %fusion.37 = f32[8,256,128]{2,1,0:T(8,128)S(1)} fusion(f32[512,256,8]{1,0,2:T(8,128)S(1)} %get-tuple-element.285, f32[8,256]{1,0:T(8,128)S(1)} %select_maximum_fusion.2, pred[256,512]{0,1:T(8,128)(4,1)S(1)} %broadcast_compare_fusion.2, f32[8,256,128]{2,1,0:T(8,128)S(1)} %get-tuple-element.304, f32[8,256]{1,0:T(8,128)S(1)} %get-tuple-element.287, ...), kind=kOutput, calls=%fused_computation.7.clone.1 | convolution fusion | flops 274464768 | bytes 6569989 | tf_op jit(solution)/shard_map/while/body/eval_jaxpr/hqk,kd->hqd/dot_general | solution.py:33
  61.0 0.1 dynamic_slice.43
  61.1 0.1 broadcast_compare_fusion.2
  61.3 0.8 fusion.34
  62.1 1.0 fusion.35
  63.1 2.6 %fusion.37 = f32[8,256,128]{2,1,0:T(8,128)S(1)} fusion(f32[512,256,8]{1,0,2:T(8,128)S(1)} %get-tuple-element.285, f32[8,256]{1,0:T(8,128)S(1)} %select_maximum_fusion.2, pred[256,512]{0,1:T(8,128)(4,1)S(1)} %broadcast_compare_fusion.2, f32[8,256,128]{2,1,0:T(8,128)S(1)} %get-tuple-element.304, f32[8,256]{1,0:T(8,128)S(1)} %get-tuple-element.287, ...), kind=kOutput, calls=%fused_computation.7.clone.1 | convolution fusion | flops 274464768 | bytes 6569989 | tf_op jit(solution)/shard_map/while/body/eval_jaxpr/hqk,kd->hqd/dot_general | solution.py:33
  65.7 0.1 dynamic_slice.43
  65.8 0.1 broadcast_compare_fusion.2
  65.9 0.8 fusion.34
  66.7 1.0 fusion.35
  67.7 2.6 %fusion.37 = f32[8,256,128]{2,1,0:T(8,128)S(1)} fusion(f32[512,256,8]{1,0,2:T(8,128)S(1)} %get-tuple-element.285, f32[8,256]{1,0:T(8,128)S(1)} %select_maximum_fusion.2, pred[256,512]{0,1:T(8,128)(4,1)S(1)} %broadcast_compare_fusion.2, f32[8,256,128]{2,1,0:T(8,128)S(1)} %get-tuple-element.304, f32[8,256]{1,0:T(8,128)S(1)} %get-tuple-element.287, ...), kind=kOutput, calls=%fused_computation.7.clone.1 | convolution fusion | flops 274464768 | bytes 6569989 | tf_op jit(solution)/shard_map/while/body/eval_jaxpr/hqk,kd->hqd/dot_general | solution.py:33
  70.3 0.1 dynamic_slice.43
  70.4 0.1 broadcast_compare_fusion.2
  70.6 0.8 fusion.34
  71.4 1.0 fusion.35
  72.4 2.6 %fusion.37 = f32[8,256,128]{2,1,0:T(8,128)S(1)} fusion(f32[512,256,8]{1,0,2:T(8,128)S(1)} %get-tuple-element.285, f32[8,256]{1,0:T(8,128)S(1)} %select_maximum_fusion.2, pred[256,512]{0,1:T(8,128)(4,1)S(1)} %broadcast_compare_fusion.2, f32[8,256,128]{2,1,0:T(8,128)S(1)} %get-tuple-element.304, f32[8,256]{1,0:T(8,128)S(1)} %get-tuple-element.287, ...), kind=kOutput, calls=%fused_computation.7.clone.1 | convolution fusion | flops 274464768 | bytes 6569989 | tf_op jit(solution)/shard_map/while/body/eval_jaxpr/hqk,kd->hqd/dot_general | solution.py:33
  75.0 0.1 dynamic_slice.43
  75.1 0.1 broadcast_compare_fusion.2
  75.2 0.8 fusion.34
  76.0 1.0 fusion.35
  77.1 2.6 %fusion.37 = f32[8,256,128]{2,1,0:T(8,128)S(1)} fusion(f32[512,256,8]{1,0,2:T(8,128)S(1)} %get-tuple-element.285, f32[8,256]{1,0:T(8,128)S(1)} %select_maximum_fusion.2, pred[256,512]{0,1:T(8,128)(4,1)S(1)} %broadcast_compare_fusion.2, f32[8,256,128]{2,1,0:T(8,128)S(1)} %get-tuple-element.304, f32[8,256]{1,0:T(8,128)S(1)} %get-tuple-element.287, ...), kind=kOutput, calls=%fused_computation.7.clone.1 | convolution fusion | flops 274464768 | bytes 6569989 | tf_op jit(solution)/shard_map/while/body/eval_jaxpr/hqk,kd->hqd/dot_general | solution.py:33
  79.7 0.1 dynamic_slice.43
  79.7 0.1 broadcast_compare_fusion.2
  79.9 0.8 fusion.34
  80.7 1.0 fusion.35
  81.7 2.6 %fusion.37 = f32[8,256,128]{2,1,0:T(8,128)S(1)} fusion(f32[512,256,8]{1,0,2:T(8,128)S(1)} %get-tuple-element.285, f32[8,256]{1,0:T(8,128)S(1)} %select_maximum_fusion.2, pred[256,512]{0,1:T(8,128)(4,1)S(1)} %broadcast_compare_fusion.2, f32[8,256,128]{2,1,0:T(8,128)S(1)} %get-tuple-element.304, f32[8,256]{1,0:T(8,128)S(1)} %get-tuple-element.287, ...), kind=kOutput, calls=%fused_computation.7.clone.1 | convolution fusion | flops 274464768 | bytes 6569989 | tf_op jit(solution)/shard_map/while/body/eval_jaxpr/hqk,kd->hqd/dot_general | solution.py:33
  84.3 0.1 dynamic_slice.43
  84.4 0.1 broadcast_compare_fusion.2
  84.5 0.8 fusion.34
  85.3 1.0 fusion.35
  86.4 2.6 %fusion.37 = f32[8,256,128]{2,1,0:T(8,128)S(1)} fusion(f32[512,256,8]{1,0,2:T(8,128)S(1)} %get-tuple-element.285, f32[8,256]{1,0:T(8,128)S(1)} %select_maximum_fusion.2, pred[256,512]{0,1:T(8,128)(4,1)S(1)} %broadcast_compare_fusion.2, f32[8,256,128]{2,1,0:T(8,128)S(1)} %get-tuple-element.304, f32[8,256]{1,0:T(8,128)S(1)} %get-tuple-element.287, ...), kind=kOutput, calls=%fused_computation.7.clone.1 | convolution fusion | flops 274464768 | bytes 6569989 | tf_op jit(solution)/shard_map/while/body/eval_jaxpr/hqk,kd->hqd/dot_general | solution.py:33
  89.0 0.1 dynamic_slice.43
  89.0 0.1 broadcast_compare_fusion.2
  89.2 0.8 fusion.34
  90.0 1.0 fusion.35
  91.0 2.6 %fusion.37 = f32[8,256,128]{2,1,0:T(8,128)S(1)} fusion(f32[512,256,8]{1,0,2:T(8,128)S(1)} %get-tuple-element.285, f32[8,256]{1,0:T(8,128)S(1)} %select_maximum_fusion.2, pred[256,512]{0,1:T(8,128)(4,1)S(1)} %broadcast_compare_fusion.2, f32[8,256,128]{2,1,0:T(8,128)S(1)} %get-tuple-element.304, f32[8,256]{1,0:T(8,128)S(1)} %get-tuple-element.287, ...), kind=kOutput, calls=%fused_computation.7.clone.1 | convolution fusion | flops 274464768 | bytes 6569989 | tf_op jit(solution)/shard_map/while/body/eval_jaxpr/hqk,kd->hqd/dot_general | solution.py:33
  93.6 1.1 %copy_bitcast_fusion = bf16[256,1024]{1,0:T(8,128)(2,1)} fusion(f32[8,256,128]{2,1,0:T(8,128)S(1)} %get-tuple-element.160, f32[8,256]{1,0:T(8,128)S(1)} %get-tuple-element.161), kind=kLoop, calls=%fused_computation.25 | loop fusion | flops 524288 | bytes 1581056 | tf_op jit(solution)/shard_map/convert_element_type | solution.py:66
  (31 shorter events, 0.3 us)
Async XLA Ops:
  6.5 47.2 %all-gather.2.cloned.1.call-start = ((), (), s32[]{:S(2)}) async-start(), calls=%async_computation | async-start | bytes 2228224 | tf_op jit(solution)/shard_map/all_gather | solution.py:49
Sparse Core Ops, SparseCore 0:
  9.5 44.1 all-gather.1
